TPU v7x, 32 devices: a whole 2x2x4 slice. The times are simulated.
32 devices in a mesh: section: 2 (over y), row: 4 (over x, core), col: 4 (over z).
Axes of the slice: x: 2, y: 2, z: 4, core: 2. Of those that a mesh axis runs over, the one named last changes fastest.
Arguments:
- inputs: float32 [3, 128, 16384], P(None, None, ('row', 'col')), may hold values from -512 to 512
- weights: float32 [2, 4, 4, 1024, 16384], P('section', None, 'col', None, 'row'), may hold values from -1 to 1
- norm_gain: float32 [2, 16384], P('section', ('row', 'col')), may hold values from 0.5 to 1.5
Outputs:
- section_outputs: float32 [2, 3, 128, 16384], P('section', None, None, ('row', 'col'))
All inputs are finite; a program needn't handle non-finite values.
Results may differ from a plain program's by a relative error of at most 0.00036.
Values sent between devices are 32-bit elements; how exact they have to be, the bound alone decides.
A program may use at most 192 MiB of HBM per device.

v0:
```python
import functools

import jax
import jax.numpy as jnp
from jax import lax
from jax.experimental import pallas as pl
from jax.experimental.pallas import tpu as pltpu
from jax.sharding import PartitionSpec as P

MESH = pl.DeviceIdType.MESH
GROUP = 16
SLOTS = 4


def slices(values):
    first = values.astype(jnp.bfloat16)
    second = (values - first.astype(jnp.float32)).astype(jnp.bfloat16)
    return first, second


def kernel(
    sections, row_count, col_count,
    x_ref, w_ref, gain_ref, out_ref,
    gathered, lhs, part, landed, active, squares, handed, handing, tiles,
    col_out, col_in, row_out, row_in,
    tile_sem, ag_send, ag_recv, rs_send, rs_recv,
    col_send, col_recv, row_send, row_recv, next_send, next_recv,
):
    micro, rows, pieces = x_ref.shape
    width = tiles.shape[2]
    per_chunk = pieces // width
    per_micro = per_chunk * col_count
    total_features = pieces * row_count * col_count
    section = lax.axis_index("section")
    row = lax.axis_index("row")
    col = lax.axis_index("col")
    cores = 2 if row_count % 2 == 0 else 1
    chips = row_count // cores
    core = lax.rem(row, cores)
    chip = row // cores

    def around(position, step, count):
        return lax.rem(position + step, count)

    def chip_row(step, which):
        return around(chip, step, chips) * cores + which

    def remote(src, dst, send, recv, device):
        return pltpu.make_async_remote_copy(
            src_ref=src, dst_ref=dst, send_sem=send, recv_sem=recv,
            device_id=device, device_id_type=MESH,
        )

    def fetch(step):
        within = lax.rem(step, per_micro)
        chunk = around(col, 1 + within // per_chunk, col_count)
        start = chunk * pieces + lax.rem(within, per_chunk) * width
        slot = lax.rem(step, SLOTS)
        return pltpu.make_async_copy(
            w_ref.at[:, pl.ds(pl.multiple_of(start, width), width)],
            tiles.at[slot], tile_sem.at[slot],
        )

    for step in range(SLOTS - 1):
        fetch(step).start()

    barrier = pltpu.get_barrier_semaphore()
    for step in range(1, row_count):
        pl.semaphore_signal(barrier, inc=1, device_id={"row": around(row, step, row_count)}, device_id_type=MESH)
    for step in range(1, col_count):
        pl.semaphore_signal(barrier, inc=1, device_id={"col": around(col, step, col_count)}, device_id_type=MESH)

    @pl.when(section > 0)
    def _():
        pl.semaphore_signal(barrier, inc=1, device_id={"section": section - 1}, device_id_type=MESH)

    @pl.when(section < sections - 1)
    def _():
        pl.semaphore_signal(barrier, inc=1, device_id={"section": section + 1}, device_id_type=MESH)

    before = (section + sections - 1) // sections
    after = (2 * (sections - 1) - section) // sections
    pl.semaphore_wait(barrier, row_count + col_count - 2 + before + after)

    def gather_send(m, source, target):
        return remote(source, gathered.at[m, row], ag_send.at[m, target], ag_recv.at[m, row], {"row": target})

    def gather_start(m, source):
        gathered[m, row] = source[...]
        for step in range(1, chips):
            gather_send(m, source, chip_row(step, core)).start()
        if cores == 2:
            gather_send(m, source, chip * cores + 1 - core).start()

    def gather_forward(m, step):
        held = chip_row(step, core)
        slot = chip_row(step, 1 - core)
        return remote(
            gathered.at[m, held], gathered.at[m, held], ag_send.at[m, slot],
            ag_recv.at[m, held], {"row": chip * cores + 1 - core},
        )

    def gather_landed(m, source):
        target = around(row, 1, row_count)
        remote(gathered.at[m, source], gathered.at[m, source], ag_send.at[m, source],
               ag_recv.at[m, source], {"row": target}).wait_recv()

    def hand(m):
        return remote(handing.at[m], handed.at[m], next_send.at[m], next_recv.at[m], {"section": section + 1})

    def chunk_send(m, chunk):
        return remote(part.at[m, chunk], landed.at[m, col], rs_send.at[m, chunk], rs_recv.at[m, col], {"col": chunk})

    @pl.when(section == 0)
    def _():
        def begin(m, carry):
            gather_start(m, x_ref.at[m])
            return carry
        lax.fori_loop(0, micro, begin, 0)

    def multiply(m):
        @pl.when(section > 0)
        def _():
            remote(handing.at[m], handed.at[m], next_send.at[m], next_recv.at[m], {"section": section - 1}).wait_recv()
            gather_start(m, handed.at[m])

        for step in range(1, chips):
            gather_landed(m, chip_row(step, core))
            if cores == 2:
                gather_forward(m, step).start()
        if cores == 2:
            for step in range(chips):
                gather_landed(m, chip_row(step, 1 - core))

        def prepare(r, carry):
            first, second = slices(gathered[m, r])
            lhs[r, :rows] = first
            lhs[r, rows:] = second
            return carry
        lax.fori_loop(0, row_count, prepare, 0)

        def chunk_body(i, carry):
            chunk = around(col, 1 + i, col_count)

            def tile_body(j, carry):
                step = m * per_micro + i * per_chunk + j
                slot = lax.rem(step, SLOTS)

                @pl.when(step + SLOTS - 1 < micro * per_micro)
                def _():
                    fetch(step + SLOTS - 1).start()

                fetch(step).wait()
                both = jnp.zeros((2 * rows, width), jnp.float32)
                low = jnp.zeros((rows, width), jnp.float32)
                for r in range(row_count):
                    first, second = slices(tiles[slot, r * pieces:(r + 1) * pieces, :])
                    both += jnp.dot(lhs[r], first, preferred_element_type=jnp.float32)
                    low += jnp.dot(lhs[r, :rows], second, preferred_element_type=jnp.float32)
                part[m, chunk, :, pl.ds(pl.multiple_of(j * width, width), width)] = both[:rows] + (both[rows:] + low)
                return carry
            lax.fori_loop(0, per_chunk, tile_body, 0)

            @pl.when(i < col_count - 1)
            def _():
                chunk_send(m, chunk).start()
            return carry
        lax.fori_loop(0, col_count, chunk_body, 0)

    def finish(m):
        for step in range(1, col_count):
            source = around(col, step, col_count)
            remote(part.at[m, source], landed.at[m, source], rs_send.at[m, source],
                   rs_recv.at[m, source], {"col": source}).wait_recv()

        def activate(g, carry):
            span = pl.ds(pl.multiple_of(g * GROUP, GROUP), GROUP)
            z = part[m, col, span, :]
            for step in range(1, col_count):
                z += landed[m, around(col, step, col_count), span, :]
            y = jax.nn.gelu(z, approximate=True)
            active[span, :] = y
            squares[span, :] = jnp.broadcast_to(jnp.sum(y * y, axis=1, keepdims=True), (GROUP, 128))
            return carry
        lax.fori_loop(0, rows // GROUP, activate, 0)

        def share(own, outgoing, incoming, send, recv, axis, position, count):
            outgoing[m] = own
            copies = []
            for step in range(1, count):
                target = around(position, step, count)
                copies.append(remote(outgoing.at[m], incoming.at[m, position], send.at[m, target],
                                     recv.at[m, position], {axis: target}))
                copies[-1].start()
            total = own
            for step in range(1, count):
                source = around(position, step, count)
                remote(outgoing.at[m], incoming.at[m, source], send.at[m, source],
                       recv.at[m, source], {axis: source}).wait_recv()
                total = total + incoming[m, source]
            for copy in copies:
                copy.wait_send()
            return total

        total = squares[...].T[:8]
        total = share(total, col_out, col_in, col_send, col_recv, "col", col, col_count)
        total = share(total, row_out, row_in, row_send, row_recv, "row", row, row_count)
        scale = lax.rsqrt(total[:1] / total_features + 1e-06)
        squares[...] = jnp.broadcast_to(scale, (128, rows)).T

        def normalize(g, carry):
            span = pl.ds(pl.multiple_of(g * GROUP, GROUP), GROUP)
            o = active[span, :] * squares[span, :1] * gain_ref[...]
            out_ref[m, span, :] = o
            handing[m, span, :] = gathered[m, row, span, :] + o
            return carry
        lax.fori_loop(0, rows // GROUP, normalize, 0)

        @pl.when(section < sections - 1)
        def _():
            hand(m).start()

    def step_body(m, carry):
        @pl.when(m < micro)
        def _():
            multiply(m)

        @pl.when(m > 0)
        def _():
            finish(m - 1)
        return carry
    lax.fori_loop(0, micro + 1, step_body, 0)

    def drain(m, carry):
        for step in range(1, chips):
            gather_send(m, x_ref.at[m], chip_row(step, core)).wait_send()
            if cores == 2:
                gather_forward(m, step).wait_send()
        if cores == 2:
            gather_send(m, x_ref.at[m], chip * cores + 1 - core).wait_send()
        for step in range(1, col_count):
            chunk_send(m, around(col, step, col_count)).wait_send()

        @pl.when(section < sections - 1)
        def _():
            hand(m).wait_send()
        return carry
    lax.fori_loop(0, micro, drain, 0)


def solution(mesh):
    sections, row_count, col_count = (mesh.shape[name] for name in ("section", "row", "col"))

    def shards(inputs, weights, norm_gain):
        micro, rows, pieces = inputs.shape
        depth = row_count * pieces
        out_cols = weights.shape[4]
        width = min(256, pieces)
        f32 = jnp.float32
        dma = pltpu.SemaphoreType.DMA
        result = pl.pallas_call(
            functools.partial(kernel, sections, row_count, col_count),
            out_shape=jax.ShapeDtypeStruct((micro, rows, pieces), f32),
            in_specs=[
                pl.BlockSpec(memory_space=pltpu.VMEM),
                pl.BlockSpec(memory_space=pltpu.HBM),
                pl.BlockSpec(memory_space=pltpu.VMEM),
            ],
            out_specs=pl.BlockSpec(memory_space=pltpu.VMEM),
            scratch_shapes=[
                pltpu.VMEM((micro, row_count, rows, pieces), f32),
                pltpu.VMEM((row_count, 2 * rows, pieces), jnp.bfloat16),
                pltpu.VMEM((micro, col_count, rows, pieces), f32),
                pltpu.VMEM((micro, col_count, rows, pieces), f32),
                pltpu.VMEM((rows, pieces), f32),
                pltpu.VMEM((rows, 128), f32),
                pltpu.VMEM((micro, rows, pieces), f32),
                pltpu.VMEM((micro, rows, pieces), f32),
                pltpu.VMEM((SLOTS, depth, width), f32),
                pltpu.VMEM((micro, 8, rows), f32),
                pltpu.VMEM((micro, col_count, 8, rows), f32),
                pltpu.VMEM((micro, 8, rows), f32),
                pltpu.VMEM((micro, row_count, 8, rows), f32),
                dma((SLOTS,)),
                dma((micro, row_count)),
                dma((micro, row_count)),
                dma((micro, col_count)),
                dma((micro, col_count)),
                dma((micro, col_count)),
                dma((micro, col_count)),
                dma((micro, row_count)),
                dma((micro, row_count)),
                dma((micro,)),
                dma((micro,)),
            ],
            compiler_params=pltpu.CompilerParams(
                collective_id=0, has_side_effects=True, vmem_limit_bytes=60 * 1024 * 1024
            ),
        )(inputs, weights.reshape(depth, out_cols), norm_gain)
        return result[None]

    placed = (
        P(None, None, ("row", "col")),
        P("section", None, "col", None, "row"),
        P("section", ("row", "col")),
    )
    return jax.shard_map(
        shards,
        mesh=mesh,
        in_specs=placed,
        out_specs=P("section", None, None, ("row", "col")),
        check_vma=False,
    )
```

profile of v0, /device:TPU:4, one launch (start us, length us, event | category | flops | bytes accessed | tf_op | source)
XLA Modules:
  0.0 341.4 jit_solution(16028113854324109294)
XLA Ops:
  0.0 338.7 %shard_map.37 = f32[3,128,1024]{2,1,0:T(8,128)} custom-call(f32[3,128,1024]{2,1,0:T(8,128)} %x_ref.1, f32[4096,4096]{1,0:T(8,128)} %bitcast.w_ref, f32[1,1024]{1,0:T(1,128)} %gain_ref.1), custom_call_target="tpu_custom_call" | custom-call | tf_op jit(solution)/shard_map/pallas_call | solution.py:261
  338.7 2.7 copy.5
where the time goes:
time: 342 us; the launch traced here: 341 us
  Pallas kernels  339 us (99%)
    pallas_call x1, Pallas kernels, shards(): pl.pallas_call(functools.partial(kernel, sections, row_count, col_count),...  339 us

commit v1 on v0

v1 whole, which is shorter than its diff:
```python
import functools

import jax
import jax.numpy as jnp
from jax import lax
from jax.experimental import pallas as pl
from jax.experimental.pallas import tpu as pltpu
from jax.sharding import PartitionSpec as P

MESH = pl.DeviceIdType.MESH
SPAN = 16
RING = 3
KEEP = 4
PARTS = 2


def slices(values):
    first = values.astype(jnp.bfloat16)
    second = (values - first.astype(jnp.float32)).astype(jnp.bfloat16)
    return first, second


def sending_order(col_count):
    table = []
    for here in range(col_count):
        keys = []
        for there in range(col_count):
            if there > here:
                keys.append((col_count - 1 - there + here, there))
            elif there < here:
                keys.append((there + col_count - 1 - here, there))
        table.append([there for _, there in sorted(keys)] + [here])
    return table


def kernel(
    sections, row_count, col_count,
    x_ref, w_ref, gain_ref, out_ref,
    gathered, branch, lhs, part, landed, scaled, squares, factor, factor_in, tiles,
    col_out, col_in, row_out, row_in,
    tile_sem, gx_send, gx_recv, gy_send, gy_recv, rs_send, rs_recv,
    col_send, col_recv, row_send, row_recv, next_send, next_recv, fac_send, fac_recv,
):
    groups, rows, pieces = x_ref.shape
    width = tiles.shape[2]
    per_chunk = pieces // width
    steps = per_chunk * col_count
    kept = steps // KEEP
    total_features = pieces * row_count * col_count
    section = lax.axis_index("section")
    row = lax.axis_index("row")
    col = lax.axis_index("col")
    cores = 2 if row_count % 2 == 0 else 1
    chips = row_count // cores
    core = lax.rem(row, cores)
    chip = row // cores
    edge = (col == 0) | (col == col_count - 1)
    inner = (col > 0) & (col < col_count - 1)
    first_section = section == 0
    table = sending_order(col_count)

    def passing(k):
        found = jnp.int32(0)
        for here in range(col_count):
            for place in range(col_count):
                found = jnp.where((col == here) & (k == place), table[here][place], found)
        return found

    def around(position, step, count):
        return lax.rem(position + step, count)

    def chip_row(step, which):
        return around(chip, step, chips) * cores + which

    def remote(src, dst, send, recv, device):
        return pltpu.make_async_remote_copy(
            src_ref=src, dst_ref=dst, send_sem=send, recv_sem=recv,
            device_id=device, device_id_type=MESH,
        )

    def slot_of(m, q):
        stream = m * (steps - kept) + q - q // KEEP - 1
        return jnp.where(lax.rem(q, KEEP) == 0, RING + q // KEEP, lax.rem(jnp.maximum(stream, 0), RING))

    def fetch(m, q):
        start = passing(q // per_chunk) * pieces + lax.rem(q, per_chunk) * width
        slot = slot_of(m, q)
        return pltpu.make_async_copy(
            w_ref.at[:, pl.ds(pl.multiple_of(start, width), width)],
            tiles.at[slot], tile_sem.at[slot],
        )

    def fetched(m, q):
        return (m == 0) | (lax.rem(q, KEEP) != 0)

    for q in range(RING):
        fetch(0, q).start()

    barrier = pltpu.get_barrier_semaphore()
    for step in range(1, row_count):
        pl.semaphore_signal(barrier, inc=1, device_id={"row": around(row, step, row_count)}, device_id_type=MESH)
    for step in range(1, col_count):
        pl.semaphore_signal(barrier, inc=1, device_id={"col": around(col, step, col_count)}, device_id_type=MESH)

    @pl.when(section > 0)
    def _():
        pl.semaphore_signal(barrier, inc=1, device_id={"section": section - 1}, device_id_type=MESH)

    @pl.when(section < sections - 1)
    def _():
        pl.semaphore_signal(barrier, inc=1, device_id={"section": section + 1}, device_id_type=MESH)

    before = (section + sections - 1) // sections
    after = (2 * (sections - 1) - section) // sections
    pl.semaphore_wait(barrier, row_count + col_count - 2 + before + after)

    def gather_send(buffer, send, recv, m, target):
        return remote(buffer.at[m, row], buffer.at[m, row], send.at[m, target], recv.at[m, row], {"row": target})

    def gather_start(buffer, send, recv, m):
        for step in range(1, chips):
            gather_send(buffer, send, recv, m, chip_row(step, core)).start()
        if cores == 2:
            gather_send(buffer, send, recv, m, chip * cores + 1 - core).start()

    def gather_forward(buffer, send, recv, m, step):
        held = chip_row(step, core)
        slot = chip_row(step, 1 - core)
        return remote(
            buffer.at[m, held], buffer.at[m, held], send.at[m, slot],
            recv.at[m, held], {"row": chip * cores + 1 - core},
        )

    def gather_landed(buffer, send, recv, m, source):
        target = around(row, 1, row_count)
        remote(buffer.at[m, source], buffer.at[m, source], send.at[m, source],
               recv.at[m, source], {"row": target}).wait_recv()

    def gather_relay(buffer, send, recv, m):
        for step in range(1, chips):
            gather_landed(buffer, send, recv, m, chip_row(step, core))
            if cores == 2:
                gather_forward(buffer, send, recv, m, step).start()

    def gather_rest(buffer, send, recv, m):
        if cores == 2:
            for step in range(chips):
                gather_landed(buffer, send, recv, m, chip_row(step, 1 - core))

    def gather_drain(buffer, send, recv, m):
        for step in range(1, chips):
            gather_send(buffer, send, recv, m, chip_row(step, core)).wait_send()
            if cores == 2:
                gather_forward(buffer, send, recv, m, step).wait_send()
        if cores == 2:
            gather_send(buffer, send, recv, m, chip * cores + 1 - core).wait_send()

    gx = (gathered, gx_send, gx_recv)
    gy = (branch, gy_send, gy_recv)

    def x_start(m):
        gathered[m, row] = x_ref[m]
        gather_start(*gx, m)

    def hand(m, target):
        return remote(scaled.at[m], branch.at[m, row], next_send.at[m], next_recv.at[m], {"section": target})

    def hand_factor(m, target):
        return remote(factor.at[m], factor_in.at[m], fac_send.at[m], fac_recv.at[m], {"section": target})

    def unit(m, there):
        upward = (there > col).astype(jnp.int32)
        slot = there + upward
        return remote(part.at[m, there], landed.at[m, slot], rs_send.at[m, there],
                      rs_recv.at[m, slot], {"col": col + 2 * upward - 1})

    def take(m, slot, there):
        remote(part.at[m, there], landed.at[m, slot], rs_send.at[m, there],
               rs_recv.at[m, slot], {"col": around(col, 1, col_count)}).wait_recv()

        def grow(g, carry):
            span = pl.ds(pl.multiple_of(g * SPAN, SPAN), SPAN)
            part[m, there, span, :] += landed[m, slot, span, :]
            return carry
        lax.fori_loop(0, rows // SPAN, grow, 0)

    def forward(m, k):
        there = passing(k)
        take(m, there + (there > col).astype(jnp.int32), there)
        unit(m, there).start()

    def issue(m, i):
        @pl.when(i > 0)
        def _():
            unit(m, passing(i - 1)).wait_send()

        @pl.when((i == 0) & (m > 0))
        def _():
            unit(m - 1, passing(col_count - 2)).wait_send()
        unit(m, passing(i)).start()

    def share_start(m, outgoing, incoming, send, recv, axis, position, count):
        for step in range(1, count):
            target = around(position, step, count)
            remote(outgoing.at[m], incoming.at[m, position], send.at[m, target],
                   recv.at[m, position], {axis: target}).start()

    def share_total(m, outgoing, incoming, send, recv, axis, position, count):
        total = outgoing[m]
        for step in range(1, count):
            source = around(position, step, count)
            remote(outgoing.at[m], incoming.at[m, source], send.at[m, source],
                   recv.at[m, source], {axis: source}).wait_recv()
            total = total + incoming[m, source]
        for step in range(1, count):
            target = around(position, step, count)
            remote(outgoing.at[m], incoming.at[m, position], send.at[m, target],
                   recv.at[m, position], {axis: target}).wait_send()
        return total

    by_row = (row_out, row_in, row_send, row_recv, "row", row, row_count)
    by_col = (col_out, col_in, col_send, col_recv, "col", col, col_count)

    def activate(m):
        @pl.when(col > 0)
        def _():
            take(m, col + 1, col)

        @pl.when(col < col_count - 1)
        def _():
            take(m, col, col)

        def spans(g, carry):
            span = pl.ds(pl.multiple_of(g * SPAN, SPAN), SPAN)
            y = jax.nn.gelu(part[m, col, span, :], approximate=True)
            scaled[m, span, :] = y * gain_ref[...]
            squares[span, :] = jnp.broadcast_to(jnp.sum(y * y, axis=1, keepdims=True), (SPAN, 128))
            return carry
        lax.fori_loop(0, rows // SPAN, spans, 0)

        @pl.when(section < sections - 1)
        def _():
            hand(m, section + 1).start()
        row_out[m] = squares[...].T[:8]
        share_start(m, *by_row)
        col_out[m] = share_total(m, *by_row)
        share_start(m, *by_col)

    def normalize(m):
        total = share_total(m, *by_col)
        scale = lax.rsqrt(total[:1] / total_features + 1e-06)
        squares[...] = jnp.broadcast_to(scale, (128, 128)).T
        factor[m] = squares[:rows]

        @pl.when(section < sections - 1)
        def _():
            hand_factor(m, section + 1).start()

        def spans(g, carry):
            span = pl.ds(pl.multiple_of(g * SPAN, SPAN), SPAN)
            out_ref[m, span, :] = scaled[m, span, :] * factor[m, span, :1]
            return carry
        lax.fori_loop(0, rows // SPAN, spans, 0)

    def prepare(m, added):
        def body(r, carry):
            lanes = pl.ds(pl.multiple_of(r * pieces, pieces), pieces)
            for start in range(0, rows, SPAN):
                values = gathered[m, r, start:start + SPAN]
                if added:
                    values = values + branch[m, r, start:start + SPAN] * factor_in[m, start:start + SPAN, :1]
                first, second = slices(values)
                lhs[start:start + SPAN, lanes] = first
                lhs[rows + start:rows + start + SPAN, lanes] = second
            return carry
        lax.fori_loop(0, row_count, body, 0)

    def acquire(m):
        @pl.when(first_section)
        def _():
            @pl.when(m == 0)
            def _():
                gather_relay(*gx, m)
            gather_rest(*gx, m)

            @pl.when(m + 1 < groups)
            def _():
                x_start(m + 1)
            prepare(m, False)

        @pl.when(section > 0)
        def _():
            @pl.when(m == 0)
            def _():
                def early(n, carry):
                    gather_relay(*gx, n)
                    gather_rest(*gx, n)
                    return carry
                lax.fori_loop(0, groups, early, 0)
                hand(m, section - 1).wait_recv()
                gather_start(*gy, m)
            gather_relay(*gy, m)
            gather_rest(*gy, m)
            hand_factor(m, section - 1).wait_recv()
            prepare(m, True)

    def multiply(m, i):
        there = passing(i)

        def tile_body(j, carry):
            q = i * per_chunk + j
            ahead = m * steps + q + RING
            ahead_m = ahead // steps
            ahead_q = lax.rem(ahead, steps)

            @pl.when((ahead < groups * steps) & fetched(ahead_m, ahead_q))
            def _():
                fetch(ahead_m, ahead_q).start()

            @pl.when(fetched(m, q))
            def _():
                fetch(m, q).wait()
            first, second = slices(tiles[slot_of(m, q)])
            both = jnp.dot(lhs[...], first, preferred_element_type=jnp.float32)
            low = jnp.dot(lhs[:rows], second, preferred_element_type=jnp.float32)
            part[m, there, :, pl.ds(pl.multiple_of(j * width, width), width)] = both[:rows] + (both[rows:] + low)
            return carry
        lax.fori_loop(0, per_chunk, tile_body, 0)

    @pl.when(first_section)
    def _():
        x_start(0)

    @pl.when(section > 0)
    def _():
        def begin(m, carry):
            x_start(m)
            return carry
        lax.fori_loop(0, groups, begin, 0)

    def group_body(m, carry):
        last = m - 1

        @pl.when(m < groups)
        def _():
            acquire(m)

        def chunk_body(i, carry):
            @pl.when(m < groups)
            def _():
                multiply(m, i)

            @pl.when((i == 0) & (m > 0) & inner)
            def _():
                def rest(k, carry):
                    forward(last, k)
                    return carry
                lax.fori_loop(2, col_count - 1, rest, 0)

            turn = jnp.where(m == 1, 0, 1)

            @pl.when((i == turn) & (m > 0))
            def _():
                activate(last)

            @pl.when((i < col_count - 1) & (m < groups) & edge)
            def _():
                issue(m, i)

            @pl.when((i >= col_count - 2) & (m < groups) & inner)
            def _():
                forward(m, i - (col_count - 2))

            @pl.when((i == turn + 1) & (m > 0))
            def _():
                normalize(last)

            @pl.when((i == col_count - 2) & (m + 1 < groups))
            def _():
                @pl.when(first_section)
                def _():
                    gather_relay(*gx, m + 1)

                @pl.when(section > 0)
                def _():
                    hand(m + 1, section - 1).wait_recv()
                    gather_start(*gy, m + 1)
            return carry
        lax.fori_loop(0, col_count, chunk_body, 0)
        return carry
    lax.fori_loop(0, groups + 1, group_body, 0)

    @pl.when(edge)
    def _():
        unit(groups - 1, passing(col_count - 2)).wait_send()

    def drain(m, carry):
        gather_drain(*gx, m)

        @pl.when(section > 0)
        def _():
            gather_drain(*gy, m)

        @pl.when(section < sections - 1)
        def _():
            hand(m, section + 1).wait_send()
            hand_factor(m, section + 1).wait_send()

        @pl.when(inner)
        def _():
            def sent(k, carry):
                unit(m, passing(k)).wait_send()
                return carry
            lax.fori_loop(0, col_count - 1, sent, 0)
        return carry
    lax.fori_loop(0, groups, drain, 0)


def solution(mesh):
    sections, row_count, col_count = (mesh.shape[name] for name in ("section", "row", "col"))

    def shards(inputs, weights, norm_gain):
        micro, batch, pieces = inputs.shape
        groups, rows = micro * PARTS, batch // PARTS
        depth = row_count * pieces
        out_cols = weights.shape[4]
        width = min(256, pieces)
        kept = (out_cols // width) // KEEP
        f32 = jnp.float32
        dma = pltpu.SemaphoreType.DMA
        result = pl.pallas_call(
            functools.partial(kernel, sections, row_count, col_count),
            out_shape=jax.ShapeDtypeStruct((groups, rows, pieces), f32),
            in_specs=[
                pl.BlockSpec(memory_space=pltpu.VMEM),
                pl.BlockSpec(memory_space=pltpu.HBM),
                pl.BlockSpec(memory_space=pltpu.VMEM),
            ],
            out_specs=pl.BlockSpec(memory_space=pltpu.VMEM),
            scratch_shapes=[
                pltpu.VMEM((groups, row_count, rows, pieces), f32),
                pltpu.VMEM((groups, row_count, rows, pieces), f32),
                pltpu.VMEM((2 * rows, depth), jnp.bfloat16),
                pltpu.VMEM((groups, col_count, rows, pieces), f32),
                pltpu.VMEM((groups, col_count + 1, rows, pieces), f32),
                pltpu.VMEM((groups, rows, pieces), f32),
                pltpu.VMEM((128, 128), f32),
                pltpu.VMEM((groups, rows, 128), f32),
                pltpu.VMEM((groups, rows, 128), f32),
                pltpu.VMEM((RING + kept, depth, width), f32),
                pltpu.VMEM((groups, 8, 128), f32),
                pltpu.VMEM((groups, col_count, 8, 128), f32),
                pltpu.VMEM((groups, 8, 128), f32),
                pltpu.VMEM((groups, row_count, 8, 128), f32),
                dma((RING + kept,)),
                dma((groups, row_count)),
                dma((groups, row_count)),
                dma((groups, row_count)),
                dma((groups, row_count)),
                dma((groups, col_count)),
                dma((groups, col_count + 1)),
                dma((groups, col_count)),
                dma((groups, col_count)),
                dma((groups, row_count)),
                dma((groups, row_count)),
                dma((groups,)),
                dma((groups,)),
                dma((groups,)),
                dma((groups,)),
            ],
            compiler_params=pltpu.CompilerParams(
                collective_id=0, has_side_effects=True, vmem_limit_bytes=67043328
            ),
        )(inputs.reshape(groups, rows, pieces), weights.reshape(depth, out_cols), norm_gain)
        return result.reshape(1, micro, batch, pieces)

    placed = (
        P(None, None, ("row", "col")),
        P("section", None, "col", None, "row"),
        P("section", ("row", "col")),
    )
    return jax.shard_map(
        shards,
        mesh=mesh,
        in_specs=placed,
        out_specs=P("section", None, None, ("row", "col")),
        check_vma=False,
    )
```

time: 342 us -> 240 us (0.70)
  Pallas kernels: 339 us -> 237 us
    pallas_call x1, Pallas kernels: 339 us -> 237 us  [shards(): pl.pallas_call(functools.partial(kernel, sections, row_count, col_count),...]
where the time goes in v1:
time: 240 us
  Pallas kernels  237 us (99%)
  local copies, waits for them, and re-layouts  2.73 us (1%)
    pallas_call x1, Pallas kernels, shards(): pl.pallas_call(functools.partial(kernel, sections, row_count, col_count),...  237 us

profile of v1, /device:TPU:4, one launch (start us, length us, event | category | flops | bytes accessed | tf_op | source)
XLA Modules:
  0.0 239.5 jit_solution(3859500495016269141)
XLA Ops:
  0.0 236.8 %shard_map.37 = f32[6,64,1024]{2,1,0:T(8,128)} custom-call(f32[6,64,1024]{2,1,0:T(8,128)} %bitcast.4, f32[4096,4096]{1,0:T(8,128)} %bitcast.1.w_ref, f32[1,1024]{1,0:T(1,128)} %gain_ref.1), custom_call_target="tpu_custom_call" | custom-call | tf_op jit(solution)/shard_map/pallas_call | solution.py:431
  236.8 2.7 %copy.5 = f32[1,3,128,1024]{3,2,1,0:T(8,128)} copy(f32[1,3,128,1024]{3,2,1,0:T(8,128)} %bitcast.3) | data formatting | bytes 3145728

commit v2 on v1

--- a/solution.py
+++ b/solution.py
@@ -12,6 +12,10 @@
 RING = 3
 KEEP = 4
 PARTS = 2
+LAG = 2
+ACT = 2
+PASS = 3
+NORM = 2
 
 
 def slices(values):
@@ -59,11 +63,17 @@
     first_section = section == 0
     table = sending_order(col_count)
 
+    places = []
+    for place in range(col_count):
+        found = jnp.int32(table[0][place])
+        for here in range(1, col_count):
+            found = jnp.where(col == here, table[here][place], found)
+        places.append(found)
+
     def passing(k):
-        found = jnp.int32(0)
-        for here in range(col_count):
-            for place in range(col_count):
-                found = jnp.where((col == here) & (k == place), table[here][place], found)
+        found = places[0]
+        for place in range(1, col_count):
+            found = jnp.where(k == place, places[place], found)
         return found
 
     def around(position, step, count):
@@ -190,13 +200,13 @@
         unit(m, there).start()
 
     def issue(m, i):
-        @pl.when(i > 0)
-        def _():
-            unit(m, passing(i - 1)).wait_send()
-
-        @pl.when((i == 0) & (m > 0))
-        def _():
-            unit(m - 1, passing(col_count - 2)).wait_send()
+        @pl.when(i >= LAG)
+        def _():
+            unit(m, passing(i - LAG)).wait_send()
+
+        @pl.when((i < LAG) & (m > 0))
+        def _():
+            unit(m - 1, passing(col_count - 1 + i - LAG)).wait_send()
         unit(m, passing(i)).start()
 
     def share_start(m, outgoing, incoming, send, recv, axis, position, count):
@@ -243,6 +253,8 @@
             hand(m, section + 1).start()
         row_out[m] = squares[...].T[:8]
         share_start(m, *by_row)
+
+    def pass_on(m):
         col_out[m] = share_total(m, *by_row)
         share_start(m, *by_col)
 
@@ -350,6 +362,10 @@
             def _():
                 multiply(m, i)
 
+            @pl.when((i < col_count - 1) & (m < groups) & edge)
+            def _():
+                issue(m, i)
+
             @pl.when((i == 0) & (m > 0) & inner)
             def _():
                 def rest(k, carry):
@@ -357,21 +373,25 @@
                     return carry
                 lax.fori_loop(2, col_count - 1, rest, 0)
 
-            turn = jnp.where(m == 1, 0, 1)
-
-            @pl.when((i == turn) & (m > 0))
+            @pl.when((i >= col_count - 2) & (m < groups) & inner)
+            def _():
+                forward(m, i - (col_count - 2))
+
+            soon = (m == 1) | (m == groups)
+
+            @pl.when((i == jnp.where(soon, 0, ACT)) & (m > 0))
             def _():
                 activate(last)
 
-            @pl.when((i < col_count - 1) & (m < groups) & edge)
-            def _():
-                issue(m, i)
-
-            @pl.when((i >= col_count - 2) & (m < groups) & inner)
-            def _():
-                forward(m, i - (col_count - 2))
-
-            @pl.when((i == turn + 1) & (m > 0))
+            @pl.when((i == jnp.where(soon, 0, PASS)) & (m > 0))
+            def _():
+                pass_on(last)
+
+            @pl.when((i == 0) & (m > 2))
+            def _():
+                normalize(m - 2)
+
+            @pl.when((i == NORM) & soon)
             def _():
                 normalize(last)
 
@@ -392,7 +412,8 @@
 
     @pl.when(edge)
     def _():
-        unit(groups - 1, passing(col_count - 2)).wait_send()
+        for i in range(LAG):
+            unit(groups - 1, passing(col_count - 2 - i)).wait_send()
 
     def drain(m, carry):
         gather_drain(*gx, m)

time: 240 us -> 224 us (0.933)
  Pallas kernels: 237 us -> 221 us
    pallas_call x1, Pallas kernels: 237 us -> 221 us  [shards(): pl.pallas_call(functools.partial(kernel, sections, row_count, col_count),...]
where the time goes in v2:
time: 224 us; the launch traced here: 223 us
  Pallas kernels  221 us (99%)
  local copies, waits for them, and re-layouts  2.73 us (1%)
    pallas_call x1, Pallas kernels, shards(): pl.pallas_call(functools.partial(kernel, sections, row_count, col_count),...  221 us

profile of v2, /device:TPU:4, one launch (start us, length us, event | category | flops | bytes accessed | tf_op | source)
XLA Modules:
  0.0 223.4 jit_solution(15186668197783195622)
XLA Ops:
  0.0 220.7 %shard_map.37 = f32[6,64,1024]{2,1,0:T(8,128)} custom-call(f32[6,64,1024]{2,1,0:T(8,128)} %bitcast.4, f32[4096,4096]{1,0:T(8,128)} %bitcast.1.w_ref, f32[1,1024]{1,0:T(1,128)} %gain_ref.1), custom_call_target="tpu_custom_call" | custom-call | tf_op jit(solution)/shard_map/pallas_call | solution.py:452
  220.7 2.7 %copy.5 = f32[1,3,128,1024]{3,2,1,0:T(8,128)} copy(f32[1,3,128,1024]{3,2,1,0:T(8,128)} %bitcast.3) | data formatting | bytes 3145728

commit v3 on v2

--- a/solution.py
+++ b/solution.py
@@ -16,6 +16,7 @@
 ACT = 2
 PASS = 3
 NORM = 2
+LATE = 2
 
 
 def slices(values):
@@ -379,6 +380,10 @@
 
             soon = (m == 1) | (m == groups)
 
+            @pl.when((i == LATE) & (m > 2))
+            def _():
+                normalize(m - 2)
+
             @pl.when((i == jnp.where(soon, 0, ACT)) & (m > 0))
             def _():
                 activate(last)
@@ -386,10 +391,6 @@
             @pl.when((i == jnp.where(soon, 0, PASS)) & (m > 0))
             def _():
                 pass_on(last)
-
-            @pl.when((i == 0) & (m > 2))
-            def _():
-                normalize(m - 2)
 
             @pl.when((i == NORM) & soon)
             def _():

time: 224 us -> 226 us (level)
    pallas_call x1, Pallas kernels: 221 us -> 223 us  [shards(): pl.pallas_call(functools.partial(kernel, sections, row_count, col_count),...]
where the time goes in v3:
time: 226 us
  Pallas kernels  223 us (99%)
  local copies, waits for them, and re-layouts  2.73 us (1%)
    pallas_call x1, Pallas kernels, shards(): pl.pallas_call(functools.partial(kernel, sections, row_count, col_count),...  223 us

profile of v3, /device:TPU:4, one launch (start us, length us, event | category | flops | bytes accessed | tf_op | source)
XLA Modules:
  0.0 226.1 jit_solution(18339474264691677269)
XLA Ops:
  0.0 223.3 %shard_map.37 = f32[6,64,1024]{2,1,0:T(8,128)} custom-call(f32[6,64,1024]{2,1,0:T(8,128)} %bitcast.4, f32[4096,4096]{1,0:T(8,128)} %bitcast.1.w_ref, f32[1,1024]{1,0:T(1,128)} %gain_ref.1), custom_call_target="tpu_custom_call" | custom-call | tf_op jit(solution)/shard_map/pallas_call | solution.py:453
  223.4 2.7 %copy.5 = f32[1,3,128,1024]{3,2,1,0:T(8,128)} copy(f32[1,3,128,1024]{3,2,1,0:T(8,128)} %bitcast.3) | data formatting | bytes 3145728
